TPU v7x, 32 devices: a whole 2x2x4 slice. The times are simulated.
32 devices in a mesh: ga: 8 (over z, x), band: 4 (over y, core).
Axes of the slice: x: 2, y: 2, z: 4, core: 2. Of those that a mesh axis runs over, the one named last changes fastest.
Arguments:
- coeffs: bfloat16 [2, 512, 40960], P(None, ('ga', 'band')), may hold values from -6 to 6
- projectors: bfloat16 [1280, 2, 40960], P(None, None, 'ga'), may hold values from -0.01953125 to 0.01953125
- block_coupling: float32 [1280, 18], replicated, may hold values from -12 to 12
- atom_counts: int32 [160], replicated, may hold values from 4 to 18, as said below
- wave_counts: int32 [8], P('ga'), may hold values from 3840 to 5120
Outputs:
- applied: bfloat16 [2, 512, 40960], P(None, ('ga', 'band'))
- band_energy: float32 [512], P(('ga', 'band'))
- total_energy: float32 [], replicated
Inputs may be any that keep to these rules, and one draw needn't show every extreme that they name: `atom_counts`: each atom has 4, 8 or 18 projectors, the counts sum to 1280 and the largest is 18.
All inputs are finite; a program needn't handle non-finite values.
Results may differ from a plain program's by a relative error of at most 0.013.
Values may be sent and summed in bfloat16 or wider, within the bound.
A program may use at most 128 MiB of HBM per device.

v0:
```python
import math
import jax
import jax.numpy as jnp
from jax import lax
from jax.sharding import PartitionSpec as P


def block_tables(atom_counts, row_ids):
    atom_ends = jnp.cumsum(atom_counts)
    atom_starts = atom_ends - atom_counts
    inside = (atom_starts[None, :] <= row_ids[:, None]) & (atom_ends[None, :] > row_ids[:, None])
    block_first = jnp.sum(jnp.where(inside, atom_starts[None, :], 0), axis=1)
    block_length = jnp.sum(jnp.where(inside, atom_counts[None, :], 0), axis=1)
    return (block_first, block_length)


def coupling_matrix(block_first, block_length, coupling_rows, column_count):
    column_ids = lax.iota(jnp.int32, column_count)
    offsets = column_ids[None, :] - block_first[:, None]
    matrix = jnp.zeros((coupling_rows.shape[0], column_count), jnp.float32)
    for offset in range(coupling_rows.shape[1]):
        hit = (offsets == offset) & (offset < block_length[:, None])
        matrix = jnp.where(hit, coupling_rows[:, offset : offset + 1], matrix)
    return matrix


def shards(coeffs, projectors, block_coupling, atom_counts, wave_counts):
    moved_bands = lax.all_to_all(coeffs, "ga", split_axis=2, concat_axis=1, tiled=True)
    own_bands = coeffs.shape[1]
    group_bands = moved_bands.shape[1]
    wave_slots = projectors.shape[2]
    proj_total_rows = projectors.shape[0]
    in_sphere = (lax.iota(jnp.int32, wave_slots) < wave_counts[0]).astype(jnp.float32)
    masked = moved_bands * in_sphere.astype(jnp.bfloat16)
    real_part = masked[0]
    imag_part = masked[1]
    stacked = jnp.concatenate(
        [jnp.concatenate([real_part, imag_part], 1), jnp.concatenate([imag_part, -real_part], 1)], 0
    )
    flat_beta = projectors.reshape(proj_total_rows, 2 * wave_slots)
    contract_last = (((1,), (1,)), ((), ()))
    contract_first = (((0,), (0,)), ((), ()))
    ga_index = lax.axis_index("ga")
    local_terms = lax.dot_general(
        flat_beta, stacked, contract_last, preferred_element_type=jnp.float32
    )
    projections = lax.psum(local_terms, "ga")
    block_first, block_length = block_tables(atom_counts, lax.iota(jnp.int32, proj_total_rows))
    matrix = coupling_matrix(block_first, block_length, block_coupling, proj_total_rows)
    coupled = jnp.dot(
        matrix, projections, precision=lax.Precision.HIGHEST, preferred_element_type=jnp.float32
    )
    energy_terms = jnp.sum(projections * coupled, axis=0)
    group_energy = (energy_terms[:group_bands] + energy_terms[group_bands:]) / proj_total_rows
    band_energy = lax.dynamic_slice_in_dim(group_energy, ga_index * own_bands, own_bands, 0)
    total_energy = lax.psum(jnp.sum(group_energy), "band")
    products = lax.dot_general(
        coupled.astype(jnp.bfloat16), flat_beta, contract_first, preferred_element_type=jnp.float32
    )
    band_total = own_bands * lax.axis_size("ga") * lax.axis_size("band")
    total_energy = total_energy / math.sqrt(band_total)
    real_out = products[:group_bands, :wave_slots] - products[group_bands:, wave_slots:]
    imag_out = products[:group_bands, wave_slots:] + products[group_bands:, :wave_slots]
    result = (jnp.stack([real_out, imag_out]) * in_sphere).astype(jnp.bfloat16)
    applied = lax.all_to_all(result, "ga", split_axis=1, concat_axis=2, tiled=True)
    return (applied, band_energy, total_energy)


def solution(mesh):
    placed = (P(None, ("ga", "band"), None), P(None, None, "ga"), P(), P(), P("ga"))
    return jax.shard_map(
        shards,
        mesh=mesh,
        in_specs=placed,
        out_specs=(P(None, ("ga", "band"), None), P(("ga", "band")), P()),
        check_vma=False,
    )
```

profile of v0, /device:TPU:0, one launch (start us, length us, event | category | flops | bytes accessed | tf_op | source)
XLA Modules:
  0.0 439.4 jit_solution(13984395675737779399)
XLA Ops:
  7.2 38.0 %copy.21 = bf16[2,16,40960]{1,0,2:T(2,128)(2,1)} copy(bf16[2,16,40960]{2,1,0:T(8,128)(2,1)} %param.5) | data formatting | bytes 5242880 | tf_op args[0]
  45.1 24.1 %reshape.129 = bf16[8,2,81920]{2,1,0:T(2,128)(2,1)} reshape(bf16[40960,2,16]{2,1,0:T(2,128)(2,1)} %bitcast.40) | data formatting | bytes 5242880
  69.2 7.3 %all-to-all-start = ((bf16[8,2,81920]{2,1,0:T(2,128)(2,1)}), bf16[8,2,81920]{2,1,0:T(2,128)(2,1)S(1)}, u32[]{:S(2)}, u32[]{:S(2)}) async-start(bf16[8,2,81920]{2,1,0:T(2,128)(2,1)} %reshape.129), calls=%async_computation | async-start | bytes 5242880 | tf_op jit(solution)/shard_map/all_to_all | solution.py:28
  76.5 0.4 all-reduce.3.cloned.1.call-start
  77.6 23.8 %copy.29 = bf16[160,8,2,5120]{3,1,2,0:T(8,128)(2,1)} copy(bf16[160,8,2,5120]{3,2,1,0:T(2,128)(2,1)} %bitcast.41) | data formatting | bytes 52428800
  101.3 34.6 %all-to-all-done = bf16[8,2,81920]{2,1,0:T(2,128)(2,1)S(1)} async-done(((bf16[8,2,81920]{2,1,0:T(2,128)(2,1)}), bf16[8,2,81920]{2,1,0:T(2,128)(2,1)S(1)}, u32[]{:S(2)}, u32[]{:S(2)}) %all-to-all-start) | async-done | bytes 2621472 | tf_op jit(solution)/shard_map/all_to_all | solution.py:28
  136.0 17.1 %reshape.130 = bf16[40960,2,16]{2,1,0:T(2,128)(2,1)} reshape(bf16[8,2,81920]{2,1,0:T(2,128)(2,1)S(1)} %all-to-all-done) | data formatting | bytes 5242880
  153.0 37.5 %copy.28 = bf16[2,16,8,5120]{3,1,2,0:T(8,128)(2,1)S(1)} copy(bf16[2,16,8,5120]{1,0,3,2:T(2,128)(2,1)} %bitcast.39) | data formatting | bytes 5242880 | tf_op jit(solution)/shard_map/all_to_all | solution.py:28
  190.5 0.3 bitcast_multiply_fusion
  190.9 0.2 slice_bitcast_fusion.1
  191.1 0.1 fusion.168
  191.2 28.8 %fusion.138 = f32[1280,256]{0,1:T(8,128)} fusion(bf16[1280,10240]{1,0:T(8,128)(2,1)} %bitcast.37, bf16[128,5120]{1,0:T(8,128)(2,1)S(1)} %fusion.168, bf16[128,5120]{1,0:T(8,128)(2,1)S(1)} %get-tuple-element.28, bf16[128,5120]{1,0:T(8,128)(2,1)S(1)} %get-tuple-element.27), kind=kOutput, calls=%fused_computation.122 | convolution fusion | flops 6731857920 | bytes 31457280 | tf_op jit(solution)/shard_map/dot_general | solution.py:44
  220.1 0.3 reduce-window.9
  220.4 0.1 slice.88
  220.5 0.1 slice_reduce_fusion.18
  220.6 0.2 slice_reduce_fusion.17
  220.9 0.3 select_reduce_fusion
  221.3 81.6 %all-reduce.3.cloned.1.call-done = f32[1280,256]{0,1:T(8,128)} async-done(((f32[1280,256]{0,1:T(8,128)}), f32[1280,256]{0,1:T(8,128)}) %all-reduce.3.cloned.1.call-update) | async-done | bytes 1310736 | tf_op jit(solution)/shard_map/psum | solution.py:47
  303.0 39.1 %fusion = f32[1280,256]{1,0:T(8,128)} fusion(f32[1280,256]{0,1:T(8,128)} %all-reduce.3.cloned.1.call-done, f32[1280]{0:T(1024)S(1)} %get-tuple-element.19, f32[1280]{0:T(1024)S(1)} %get-tuple-element.20, f32[1280]{0:T(1024)S(1)} %get-tuple-element.4, f32[1280]{0:T(1024)S(1)} %get-tuple-element.5, f32[1280]{0:T(1024)S(1)} %get-tuple-element.6, ...), kind=kOutput, calls=%fused_computation | convolution fusion | flops 5123276800 | bytes 2741760 | tf_op jit(solution)/shard_map/dot_general | solution.py:50
  342.1 13.0 %fusion.144 = f32[256,10240]{1,0:T(8,128)S(1)} fusion(bf16[1280,10240]{1,0:T(8,128)(2,1)} %bitcast.38, f32[1280,256]{1,0:T(8,128)} %fusion), kind=kOutput, calls=%fused_computation.136 | convolution fusion | flops 6711214080 | bytes 38010880 | tf_op jit(solution)/shard_map/dot_general | solution.py:57
  355.1 0.8 fusion.142
  355.9 0.5 fusion.81
  356.4 4.2 copy.24
  360.6 3.7 all-to-all-start.1
  364.2 2.8 copy.26
  367.0 1.9 multiply_reduce_fusion
  368.9 0.6 fusion.169
  369.5 7.3 %psum.15 = f32[]{:T(128)} all-reduce(f32[]{:T(128)} %get-tuple-element.23), channel_id=1, replica_groups=mesh['ga'=8,'band'=4] {'band'}, use_global_device_ids=true, to_apply=%region_7.8 | all-reduce | flops 1 | bytes 8 | tf_op jit(solution)/shard_map/psum | solution.py:56
  376.9 0.6 dynamic_slice.3
  378.1 45.7 %all-to-all-done.1 = bf16[2,128,5120]{2,0,1:T(2,128)(2,1)S(1)} async-done(((bf16[2,128,5120]{2,0,1:T(2,128)(2,1)}), bf16[2,128,5120]{2,0,1:T(2,128)(2,1)S(1)}, u32[]{:S(2)}, u32[]{:S(2)}) %all-to-all-start.1) | async-done | bytes 2621472 | tf_op jit(solution)/shard_map/all_to_all | solution.py:65
  423.8 2.9 copy.25
  426.7 4.5 %all_to_all.33 = bf16[2,16,40960]{2,1,0:T(8,128)(2,1)} reshape(bf16[2,16,8,5120]{3,2,1,0:T(8,128)(2,1)} %copy.25) | data formatting | bytes 5242880 | tf_op jit(solution)/shard_map/all_to_all | solution.py:65
  (11 shorter events, 0.2 us)
Async XLA Ops:
  69.2 66.8 %all-to-all-start = ((bf16[8,2,81920]{2,1,0:T(2,128)(2,1)}), bf16[8,2,81920]{2,1,0:T(2,128)(2,1)S(1)}, u32[]{:S(2)}, u32[]{:S(2)}) async-start(bf16[8,2,81920]{2,1,0:T(2,128)(2,1)} %reshape.129), calls=%async_computation | async-start | bytes 5242880 | tf_op jit(solution)/shard_map/all_to_all | solution.py:28
  76.5 226.5 %all-reduce.3.cloned.1.call-start = ((), (), s32[]{:S(2)}) async-start(), calls=%async_computation.2 | async-start | bytes 2621440 | tf_op jit(solution)/shard_map/psum | solution.py:47
  191.2 28.9 %copy-start.1 = (s32[160]{0:T(256)S(1)}, s32[160]{0:T(256)}, u32[]{:S(2)}) copy-start(s32[160]{0:T(256)} %param.8) | copy-start | bytes 1924
  191.2 29.4 %copy-start = (f32[1280,18]{0,1:T(8,128)S(1)}, f32[1280,18]{0,1:T(8,128)}, u32[]{:S(2)}) copy-start(f32[1280,18]{0,1:T(8,128)} %param.7) | copy-start | bytes 276484
  360.6 63.2 %all-to-all-start.1 = ((bf16[2,128,5120]{2,0,1:T(2,128)(2,1)}), bf16[2,128,5120]{2,0,1:T(2,128)(2,1)S(1)}, u32[]{:S(2)}, u32[]{:S(2)}) async-start(bf16[2,128,5120]{2,0,1:T(2,128)(2,1)} %copy.24), calls=%async_computation.1 | async-start | bytes 5242880 | tf_op jit(solution)/shard_map/all_to_all | solution.py:65
Sparse Core Ops, SparseCore 0:
  220.2 82.7 all-reduce.2
where the time goes:
time: 447 us; the launch traced here: 439 us
  waiting for transfers between devices  162 us (36%)
  local copies, waits for them, and re-layouts  156 us (35%)
  matrix products  81 us (18%)
  between operations  16.8 us (4%)
  starting transfers between devices  11.4 us (3%)
  blocking collectives  7.33 us (2%)
  other arithmetic  4.94 us (1%)
    unnamed x8, local copies, waits for them, and re-layouts  103 us
    psum x1, waiting for transfers between devices, shards(): projections = lax.psum(local_terms, 'ga')  81.6 us
    all_to_all x1, waiting for transfers between devices, shards(): lax.all_to_all(result, 'ga', split_axis=1, concat_axis=2, tiled=True)  45.7 us
    dot_general x1, matrix products, shards(): jnp.dot(matrix, projections, precision=lax.Precision.HIGHEST, preferred_e...  39.1 us
    all_to_all x1, local copies, waits for them, and re-layouts, shards(): lax.all_to_all(coeffs, 'ga', split_axis=2, concat_axis=1, tiled=True)  37.5 us
    all_to_all x1, waiting for transfers between devices, shards(): lax.all_to_all(coeffs, 'ga', split_axis=2, concat_axis=1, tiled=True)  34.6 us
    dot_general x1, matrix products, shards(): lax.dot_general(flat_beta, stacked, contract_last, preferred_element_type...  28.8 us
    dot_general x1, matrix products, shards(): lax.dot_general(coupled.astype(jnp.bfloat16), flat_beta, contract_first,...  13 us
  transfers between devices with their start and end apart: 3, of which 3 were waited for; matrix products, arithmetic and copies ran while one was open for 7% of the time, Pallas kernels for 0%

commit v1 on v0

--- a/solution.py
+++ b/solution.py
@@ -62,7 +62,10 @@
     real_out = products[:group_bands, :wave_slots] - products[group_bands:, wave_slots:]
     imag_out = products[:group_bands, wave_slots:] + products[group_bands:, :wave_slots]
     result = (jnp.stack([real_out, imag_out]) * in_sphere).astype(jnp.bfloat16)
-    applied = lax.all_to_all(result, "ga", split_axis=1, concat_axis=2, tiled=True)
+    applied = jnp.concatenate(
+        lax.all_to_all(jnp.stack(jnp.split(result, lax.axis_size("ga"), axis=1)), "ga", 0, 0),
+        axis=2,
+    )
     return (applied, band_energy, total_energy)
 
 

time: 447 us -> 430 us (0.962)
  matrix products: 81 us -> 71.2 us
    dot_general x1, matrix products: 39.1 us -> 29.3 us  [shards(): jnp.dot(matrix, projections, precision=lax.Precision.HIGHEST, preferred_e...]
    all_to_all x2 -> x0, local copies, waits for them, and re-layouts: 7.43 us -> none  [shards(): lax.all_to_all(result, 'ga', split_axis=1, concat_axis=2, tiled=True)]
    unnamed x8 -> x15, local copies, waits for them, and re-layouts: 103 us -> 108 us
where the time goes in v1:
time: 430 us; the launch traced here: 425 us
  waiting for transfers between devices  162 us (38%)
  local copies, waits for them, and re-layouts  152 us (35%)
  matrix products  71.2 us (17%)
  between operations  16.6 us (4%)
  starting transfers between devices  11.2 us (3%)
  blocking collectives  7.34 us (2%)
  other arithmetic  4.95 us (1%)
    unnamed x15, local copies, waits for them, and re-layouts  108 us
    psum x1, waiting for transfers between devices, shards(): projections = lax.psum(local_terms, 'ga')  81.6 us
    all_to_all x1, waiting for transfers between devices, shards(): lax.all_to_all(jnp.stack(jnp.split(result, lax.axis_size('ga'), axis=1)),...  45.7 us
    all_to_all x1, local copies, waits for them, and re-layouts, shards(): lax.all_to_all(coeffs, 'ga', split_axis=2, concat_axis=1, tiled=True)  37.5 us
    all_to_all x1, waiting for transfers between devices, shards(): lax.all_to_all(coeffs, 'ga', split_axis=2, concat_axis=1, tiled=True)  34.8 us
    dot_general x1, matrix products, shards(): jnp.dot(matrix, projections, precision=lax.Precision.HIGHEST, preferred_e...  29.3 us
    dot_general x1, matrix products, shards(): lax.dot_general(flat_beta, stacked, contract_last, preferred_element_type...  28.8 us
    dot_general x1, matrix products, shards(): lax.dot_general(coupled.astype(jnp.bfloat16), flat_beta, contract_first,...  13 us
  transfers between devices with their start and end apart: 3, of which 3 were waited for; matrix products, arithmetic and copies ran while one was open for 7% of the time, Pallas kernels for 0%

profile of v1, /device:TPU:0, one launch (start us, length us, event | category | flops | bytes accessed | tf_op | source)
XLA Modules:
  0.0 425.4 jit_solution(17539805202780796367)
XLA Ops:
  7.2 38.0 %copy.19 = bf16[2,16,40960]{1,0,2:T(2,128)(2,1)} copy(bf16[2,16,40960]{2,1,0:T(8,128)(2,1)} %param.5) | data formatting | bytes 5242880 | tf_op args[0]
  45.1 24.1 %reshape.137 = bf16[8,2,81920]{2,1,0:T(2,128)(2,1)} reshape(bf16[40960,2,16]{2,1,0:T(2,128)(2,1)} %bitcast.70) | data formatting | bytes 5242880
  69.2 7.3 %all-to-all-start = ((bf16[8,2,81920]{2,1,0:T(2,128)(2,1)}), bf16[8,2,81920]{2,1,0:T(2,128)(2,1)S(1)}, u32[]{:S(2)}, u32[]{:S(2)}) async-start(bf16[8,2,81920]{2,1,0:T(2,128)(2,1)} %reshape.137), calls=%async_computation | async-start | bytes 5242880 | tf_op jit(solution)/shard_map/all_to_all | solution.py:28
  77.4 23.8 %copy.27 = bf16[160,8,2,5120]{3,1,2,0:T(8,128)(2,1)} copy(bf16[160,8,2,5120]{3,2,1,0:T(2,128)(2,1)} %bitcast.71) | data formatting | bytes 52428800
  101.2 34.8 %all-to-all-done = bf16[8,2,81920]{2,1,0:T(2,128)(2,1)S(1)} async-done(((bf16[8,2,81920]{2,1,0:T(2,128)(2,1)}), bf16[8,2,81920]{2,1,0:T(2,128)(2,1)S(1)}, u32[]{:S(2)}, u32[]{:S(2)}) %all-to-all-start) | async-done | bytes 2621472 | tf_op jit(solution)/shard_map/all_to_all | solution.py:28
  136.0 17.1 %reshape.138 = bf16[40960,2,16]{2,1,0:T(2,128)(2,1)} reshape(bf16[8,2,81920]{2,1,0:T(2,128)(2,1)S(1)} %all-to-all-done) | data formatting | bytes 5242880
  153.0 37.5 %copy.25 = bf16[2,16,8,5120]{3,1,2,0:T(8,128)(2,1)S(1)} copy(bf16[2,16,8,5120]{1,0,3,2:T(2,128)(2,1)} %bitcast.69) | data formatting | bytes 5242880 | tf_op jit(solution)/shard_map/all_to_all | solution.py:28
  190.5 0.3 bitcast_multiply_fusion
  191.2 28.8 %fusion.138 = f32[1280,256]{0,1:T(8,128)} fusion(bf16[1280,10240]{1,0:T(8,128)(2,1)} %bitcast.67, bf16[128,5120]{1,0:T(8,128)(2,1)S(1)} %fusion.176, bf16[128,5120]{1,0:T(8,128)(2,1)S(1)} %get-tuple-element.28, bf16[128,5120]{1,0:T(8,128)(2,1)S(1)} %get-tuple-element.27), kind=kOutput, calls=%fused_computation.122 | convolution fusion | flops 6731857920 | bytes 31457280 | tf_op jit(solution)/shard_map/dot_general | solution.py:44
  220.1 0.3 reduce-window.9
  220.9 0.3 select_reduce_fusion
  221.3 81.6 %all-reduce.3.cloned.1.call-done = f32[1280,256]{0,1:T(8,128)} async-done(((f32[1280,256]{0,1:T(8,128)}), f32[1280,256]{0,1:T(8,128)}) %all-reduce.3.cloned.1.call-update) | async-done | bytes 1310736 | tf_op jit(solution)/shard_map/psum | solution.py:47
  303.0 29.3 %fusion = f32[1280,256]{1,0:T(8,128)} fusion(f32[1280,256]{0,1:T(8,128)} %all-reduce.3.cloned.1.call-done, f32[1280]{0:T(1024)S(1)} %get-tuple-element.19, f32[1280]{0:T(1024)S(1)} %get-tuple-element.20, f32[1280]{0:T(1024)S(1)} %get-tuple-element.4, f32[1280]{0:T(1024)S(1)} %get-tuple-element.5, f32[1280]{0:T(1024)S(1)} %get-tuple-element.6, ...), kind=kOutput, calls=%fused_computation | convolution fusion | flops 5123276800 | bytes 2741760 | tf_op jit(solution)/shard_map/dot_general | solution.py:50
  332.3 13.0 %fusion.144 = f32[256,10240]{1,0:T(8,128)S(1)} fusion(bf16[1280,10240]{1,0:T(8,128)(2,1)} %bitcast.68, f32[1280,256]{1,0:T(8,128)} %fusion), kind=kOutput, calls=%fused_computation.136 | convolution fusion | flops 6711214080 | bytes 38010880 | tf_op jit(solution)/shard_map/dot_general | solution.py:57
  345.3 0.8 fusion.142
  346.1 0.5 fusion.81
  346.5 0.7 fusion.153
  347.3 0.7 fusion.152
  348.0 0.7 fusion.151
  348.8 0.7 fusion.150
  349.5 0.7 fusion.149
  350.3 0.7 fusion.148
  351.0 0.7 fusion.147
  351.8 0.7 fusion.146
  352.5 3.7 all-to-all-start.1
  356.2 2.8 copy.23
  359.0 1.9 multiply_reduce_fusion
  360.9 0.6 fusion.177
  361.5 7.3 %psum.15 = f32[]{:T(128)} all-reduce(f32[]{:T(128)} %get-tuple-element.23), channel_id=1, replica_groups=mesh['ga'=8,'band'=4] {'band'}, use_global_device_ids=true, to_apply=%region_7.8 | all-reduce | flops 1 | bytes 8 | tf_op jit(solution)/shard_map/psum | solution.py:56
  368.8 0.6 dynamic_slice.3
  370.1 45.7 %all-to-all-done.1 = bf16[8,2,16,5120]{3,2,1,0:T(8,128)(2,1)S(1)} async-done(((bf16[8,2,16,5120]{3,2,1,0:T(8,128)(2,1)}), bf16[8,2,16,5120]{3,2,1,0:T(8,128)(2,1)S(1)}, u32[]{:S(2)}, u32[]{:S(2)}) %all-to-all-start.1) | async-done | bytes 2621472 | tf_op jit(solution)/shard_map/all_to_all | solution.py:66
  415.7 1.7 copy.26
  (17 shorter events, 1.1 us)
Async XLA Ops:
  69.2 66.8 %all-to-all-start = ((bf16[8,2,81920]{2,1,0:T(2,128)(2,1)}), bf16[8,2,81920]{2,1,0:T(2,128)(2,1)S(1)}, u32[]{:S(2)}, u32[]{:S(2)}) async-start(bf16[8,2,81920]{2,1,0:T(2,128)(2,1)} %reshape.137), calls=%async_computation | async-start | bytes 5242880 | tf_op jit(solution)/shard_map/all_to_all | solution.py:28
  76.5 226.5 %all-reduce.3.cloned.1.call-start = ((), (), s32[]{:S(2)}) async-start(), calls=%async_computation.2 | async-start | bytes 2621440 | tf_op jit(solution)/shard_map/psum | solution.py:47
  191.2 28.9 %copy-start.1 = (s32[160]{0:T(256)S(1)}, s32[160]{0:T(256)}, u32[]{:S(2)}) copy-start(s32[160]{0:T(256)} %param.8) | copy-start | bytes 1924
  191.2 29.4 %copy-start = (f32[1280,18]{0,1:T(8,128)S(1)}, f32[1280,18]{0,1:T(8,128)}, u32[]{:S(2)}) copy-start(f32[1280,18]{0,1:T(8,128)} %param.7) | copy-start | bytes 276484
  352.5 63.2 %all-to-all-start.1 = ((bf16[8,2,16,5120]{3,2,1,0:T(8,128)(2,1)}), bf16[8,2,16,5120]{3,2,1,0:T(8,128)(2,1)S(1)}, u32[]{:S(2)}, u32[]{:S(2)}) async-start(bf16[8,2,16,5120]{3,2,1,0:T(8,128)(2,1)} %fusion.146), calls=%async_computation.1 | async-start | bytes 5242880 | tf_op jit(solution)/shard_map/all_to_all | solution.py:66
Sparse Core Ops, SparseCore 0:
  220.2 82.7 all-reduce.2
